TPU v7x, 128 devices: a whole 4x4x4 slice. The times are simulated.
128 devices in a mesh: dp: 8 (over z, y_lo), tensor: 16 (over x, y_hi, core).
Axes of the slice: x: 4, y: 4 (y_hi: 2, y_lo: 2; y = y_hi * 2 + y_lo), z: 4, core: 2. Of those that a mesh axis runs over, the one named last changes fastest.
Arguments:
- projected: bfloat16 [2, 16384, 4608], P(None, ('dp', 'tensor')), may hold values from -60 to 60
- out_grad: bfloat16 [2, 16384, 4608], P(None, ('dp', 'tensor')), may hold values from -20 to 20
- attention: bfloat16 [2, 16384, 4096], P(None, 'dp', 'tensor'), may hold values from -6 to 6
- w_out: bfloat16 [4096, 4608], P('tensor'), may hold values from -0.09375 to 0.09375
- gains: float32 [4608], replicated, may hold values from 0.5 to 1.5
- main_out: float32 [4096, 4608], P('tensor', 'dp'), may hold values from -6 to 6
- main_gains: float32 [4608], replicated, may hold values from -6 to 6
Outputs:
- attn_grad: bfloat16 [2, 16384, 4096], P(None, 'dp', 'tensor')
- new_main_out: float32 [4096, 4608], P('tensor', 'dp')
- new_main_gains: float32 [4608], replicated
All inputs are finite; a program needn't handle non-finite values.
Results may differ from a plain program's by a relative error of at most 0.0049.
Values may be sent and summed in bfloat16 or wider, within the bound.
No kernel may reach another device: no remote copies, remote signals or barrier semaphores. Data moves between devices by JAX's collectives and lax.ppermute only.
A program may use at most 128 MiB of HBM per device.

v0:
```python
import functools
import math
import jax
import jax.numpy as jnp
from jax import lax
from jax.sharding import Mesh
from jax.sharding import PartitionSpec as P

DP = ("dp_0", "dp_1")
TENSOR = ("tensor_0", "tensor_1", "tensor_2")
DP_TENSOR = ("dp_0", "dp_1", "tensor_0", "tensor_1", "tensor_2")


def by_axis(value, axes):
    return functools.reduce(lax.psum, axes, value)


def cut_along(value, dim, size):
    before, after = (value.shape[:dim], value.shape[dim + 1 :])
    return jnp.moveaxis(value.reshape(*before, size, -1, *after), dim, 0)


def sent_and_summed(value, axis, dim):
    size = lax.axis_size(axis)
    parts = lax.all_to_all(cut_along(value, dim, size), axis, 0, 0, tiled=True)
    return jnp.sum(parts.astype(jnp.float32), axis=0)


def normalized(values):
    inverse = lax.rsqrt(jnp.mean(values * values, axis=-1, keepdims=True) + 1e-06)
    return (values * inverse, inverse)


def norm_back(upstream, normed, inverse):
    return inverse * (upstream - normed * jnp.mean(upstream * normed, axis=-1, keepdims=True))


def per_device(projected, out_grad, attention, w_out, gains, main_out, main_gains):
    micro_count = projected.shape[0]
    own_rows = projected.shape[1]
    tokens_all = micro_count * own_rows * lax.axis_size(DP) * lax.axis_size(TENSOR)
    factor = 1.0 / math.sqrt(tokens_all)
    gain_total = jnp.zeros(gains.shape, jnp.float32)
    back_list = []
    for micro_step in range(micro_count):
        output_in = projected[micro_step].astype(jnp.float32)
        upstream = out_grad[micro_step].astype(jnp.float32)
        out_hat, out_inv = normalized(output_in)
        out_gain = jnp.sum(upstream * out_hat, axis=0)
        out_back = norm_back(upstream * gains, out_hat, out_inv).astype(jnp.bfloat16)
        back_list.append(out_back)
        gain_total = gain_total + by_axis(out_gain, DP_TENSOR)
    stacked = jnp.stack(back_list)
    section = lax.all_gather(stacked, TENSOR, axis=1, tiled=True)
    weight_sum = lax.dot_general(
        attention, section, (((0, 1), (0, 1)), ((), ())), preferred_element_type=jnp.float32
    )
    product = lax.dot_general(
        section, w_out, (((2,), (1,)), ((), ())), preferred_element_type=jnp.float32
    ).astype(jnp.bfloat16)
    shard_out = sent_and_summed(weight_sum.astype(jnp.bfloat16), DP, 1)
    return (product, main_out + factor * shard_out, main_gains + factor * gain_total)


def solution(mesh):
    torus = Mesh(
        mesh.devices.reshape(4, 2, 4, 2, 2), ("dp_0", "dp_1", "tensor_0", "tensor_1", "tensor_2")
    )
    return jax.shard_map(
        per_device,
        mesh=torus,
        in_specs=(
            P(None, DP_TENSOR, None),
            P(None, DP_TENSOR, None),
            P(None, DP, TENSOR),
            P(TENSOR, None),
            P(),
            P(TENSOR, DP),
            P(),
        ),
        out_specs=(P(None, DP, TENSOR), P(TENSOR, DP), P()),
        check_vma=False,
    )
```

profile of v0, /device:TPU:1, one launch (start us, length us, event | category | flops | bytes accessed | tf_op | source)
XLA Modules:
  0.0 289.6 jit_solution(4183304599025154800)
XLA Ops:
  7.2 0.0 copy-start
  7.2 0.0 all-gather.2.cloned.1.call-start
  7.2 0.0 copy-start.1
  7.2 2.3 fusion.21
  9.6 0.2 copy-done.1
  9.8 0.0 copy-start.2
  9.8 0.0 copy-start.4
  9.8 3.5 %fusion.12 = (f32[128]{0:T(128)S(1)}, f32[128]{0:T(128)S(1)}, f32[4608]{0:T(1024)S(1)}, f32[4608]{0:T(1024)S(1)}) fusion(f32[128]{0:T(128)S(1)} %get-tuple-element.12, f32[4608]{0:T(1024)} %param.11, bf16[2,128,4608]{2,1,0:T(8,128)(2,1)} %param.8, bf16[2,128,4608]{2,1,0:T(8,128)(2,1)S(1)} %copy-done.1, f32[128]{0:T(128)S(1)} %get-tuple-element.11), kind=kLoop, calls=%fused_computation.23 | loop fusion | flops 9427712 | bytes 4775936 | tf_op jit(solution)/shard_map/reduce_sum | solution.py:35
  13.2 0.0 copy-done.2
  13.2 0.0 copy-done.4
  13.3 1.4 fusion.16
  14.7 1.6 pad_maximum_fusion
  16.3 0.0 copy-start.5
  16.3 0.0 all-gather.2.cloned.1.call-update
  16.3 15.3 %psum.84 = f32[4608]{0:T(1024)S(1)} all-reduce(f32[4608]{0:T(1024)S(1)} %add.48), channel_id=1, replica_groups=mesh['dp_0'=4,'dp_1'=2,'tensor_0'=4,'tensor_1'=2,'tensor_2'=2] {'dp_0'}, use_global_device_ids=true, to_apply=%region_6.0 | all-reduce | flops 4608 | bytes 36864 | tf_op jit(solution)/shard_map/psum | solution.py:15
  31.7 7.9 %psum.83 = f32[4608]{0:T(1024)S(1)} all-reduce(f32[4608]{0:T(1024)S(1)} %psum.84), channel_id=1, replica_groups=mesh['dp_0'=4,'dp_1'=2,'tensor_0'=4,'tensor_1'=2,'tensor_2'=2] {'dp_1'}, use_global_device_ids=true, to_apply=%region_7.0 | all-reduce | flops 4608 | bytes 36864 | tf_op jit(solution)/shard_map/psum | solution.py:15
  39.6 16.0 %psum.82 = f32[4608]{0:T(1024)S(1)} all-reduce(f32[4608]{0:T(1024)S(1)} %psum.83), channel_id=1, replica_groups=mesh['dp_0'=4,'dp_1'=2,'tensor_0'=4,'tensor_1'=2,'tensor_2'=2] {'tensor_0'}, use_global_device_ids=true, to_apply=%region_8.0 | all-reduce | flops 4608 | bytes 36864 | tf_op jit(solution)/shard_map/psum | solution.py:15
  55.5 9.5 %psum.81 = f32[4608]{0:T(1024)S(1)} all-reduce(f32[4608]{0:T(1024)S(1)} %psum.82), channel_id=1, replica_groups=mesh['dp_0'=4,'dp_1'=2,'tensor_0'=4,'tensor_1'=2,'tensor_2'=2] {'tensor_1'}, use_global_device_ids=true, to_apply=%region_9.0 | all-reduce | flops 4608 | bytes 36864 | tf_op jit(solution)/shard_map/psum | solution.py:15
  65.1 12.5 %psum.80 = f32[4608]{0:T(1024)S(1)} all-reduce(f32[4608]{0:T(1024)S(1)} %psum.81), channel_id=1, replica_groups=mesh['dp_0'=4,'dp_1'=2,'tensor_0'=4,'tensor_1'=2,'tensor_2'=2] {'tensor_2'}, use_global_device_ids=true, to_apply=%region_10.0 | all-reduce | flops 4608 | bytes 36864 | tf_op jit(solution)/shard_map/psum | solution.py:15
  77.5 0.0 copy-done.5
  77.5 0.6 multiply_add_fusion.1
  78.2 149.1 %all-gather.2.cloned.1.call-done = bf16[2,2048,4608]{2,1,0:T(8,128)(2,1)} async-done(((bf16[2,128,4608]{2,1,0:T(8,128)(2,1)}), bf16[2,2048,4608]{2,1,0:T(8,128)(2,1)}) %all-gather.2.cloned.1.call-update) | async-done | bytes 37748752 | tf_op jit(solution)/shard_map/all_gather | solution.py:54
  227.2 18.6 %fusion = bf16[4608,256]{1,0:T(8,128)(2,1)} fusion(bf16[2,2048,4608]{2,1,0:T(8,128)(2,1)} %all-gather.2.cloned.1.call-done, bf16[2,2048,256]{2,1,0:T(8,128)(2,1)} %param.9), kind=kOutput, calls=%fused_computation.1 | convolution fusion | flops 9664856064 | bytes 42205184 | tf_op jit(solution)/shard_map/dot_general | solution.py:55
  245.9 4.6 %all-to-all-start = ((bf16[8,256,576]{1,2,0:T(8,128)(2,1)}), bf16[8,256,576]{1,2,0:T(8,128)(2,1)}, u32[]{:S(2)}, u32[]{:S(2)}) async-start(bf16[8,256,576]{1,2,0:T(8,128)(2,1)} %bitcast.67), calls=%async_computation | async-start | bytes 4718592 | tf_op jit(solution)/shard_map/all_to_all | solution.py:25
  250.4 0.0 copy-done
  250.5 17.8 %convolution_convert_fusion = bf16[2,2048,256]{2,1,0:T(8,128)(2,1)} fusion(bf16[2,2048,4608]{2,1,0:T(8,128)(2,1)} %all-gather.2.cloned.1.call-done, bf16[256,4608]{1,0:T(8,128)(2,1)S(1)} %copy-done), kind=kOutput, calls=%fused_computation.3 | convolution fusion | flops 9664724992 | bytes 42205184 | tf_op jit(solution)/shard_map/dot_general | solution.py:58
  268.2 0.0 copy-start.3
  268.2 11.5 %all-to-all-done = bf16[8,256,576]{1,2,0:T(8,128)(2,1)} async-done(((bf16[8,256,576]{1,2,0:T(8,128)(2,1)}), bf16[8,256,576]{1,2,0:T(8,128)(2,1)}, u32[]{:S(2)}, u32[]{:S(2)}) %all-to-all-start) | async-done | bytes 2359328 | tf_op jit(solution)/shard_map/all_to_all | solution.py:25
  279.8 2.0 convert_reduce_fusion
  281.8 0.0 copy-done.3
  281.8 0.9 multiply_add_fusion
  (4 shorter events, 0.0 us)
Async XLA Ops:
  7.2 243.3 %copy-start = (bf16[256,4608]{1,0:T(8,128)(2,1)S(1)}, bf16[256,4608]{1,0:T(8,128)(2,1)}, u32[]{:S(2)}) copy-start(bf16[256,4608]{1,0:T(8,128)(2,1)} %param.10) | copy-start | bytes 7077892
  7.2 220.1 %all-gather.2.cloned.1.call-start = ((), (), s32[]{:S(2)}) async-start(), calls=%async_computation.1 | async-start | bytes 40108032 | tf_op jit(solution)/shard_map/all_gather | solution.py:54
  7.2 2.5 copy-start.1
  9.8 3.5 %copy-start.2 = (bf16[2,128,4608]{2,1,0:T(8,128)(2,1)S(1)}, bf16[2,128,4608]{2,1,0:T(8,128)(2,1)}, u32[]{:S(2)}) copy-start(bf16[2,128,4608]{2,1,0:T(8,128)(2,1)} %param.8) | copy-start | bytes 7077892
  9.8 3.5 %copy-start.4 = (f32[4608]{0:T(1024)S(1)}, f32[4608]{0:T(1024)}, u32[]{:S(2)}) copy-start(f32[4608]{0:T(1024)} %param.11) | copy-start | bytes 55300
  16.3 61.2 %copy-start.5 = (f32[4608]{0:T(1024)S(1)}, f32[4608]{0:T(1024)}, u32[]{:S(2)}) copy-start(f32[4608]{0:T(1024)} %param.13) | copy-start | bytes 55300
  245.9 33.9 %all-to-all-start = ((bf16[8,256,576]{1,2,0:T(8,128)(2,1)}), bf16[8,256,576]{1,2,0:T(8,128)(2,1)}, u32[]{:S(2)}, u32[]{:S(2)}) async-start(bf16[8,256,576]{1,2,0:T(8,128)(2,1)} %bitcast.67), calls=%async_computation | async-start | bytes 4718592 | tf_op jit(solution)/shard_map/all_to_all | solution.py:25
  268.2 13.6 %copy-start.3 = (f32[256,576]{0,1:T(8,128)S(1)}, f32[256,576]{0,1:T(8,128)}, u32[]{:S(2)}) copy-start(f32[256,576]{0,1:T(8,128)} %param.12) | copy-start | bytes 1769476
Sparse Core Ops, SparseCore 0:
  16.5 210.7 all-gather.1
where the time goes:
time: 290 us
  waiting for transfers between devices  161 us (56%)
  blocking collectives  61.2 us (21%)
  matrix products  36.4 us (13%)
  between operations  14.1 us (5%)
  other arithmetic  12.4 us (4%)
  starting transfers between devices  4.6 us (2%)
    all_gather x1, waiting for transfers between devices, per_device(): section = lax.all_gather(stacked, TENSOR, axis=1, tiled=True)  149 us
    psum x5, blocking collectives, by_axis(): return functools.reduce(lax.psum, axes, value)  61.2 us
    dot_general x1, matrix products, per_device(): lax.dot_general(attention, section, (((0, 1), (0, 1)), ((), ())), preferr...  18.6 us
    dot_general x1, matrix products, per_device(): lax.dot_general(section, w_out, (((2,), (1,)), ((), ())), preferred_eleme...  17.8 us
    all_to_all x1, waiting for transfers between devices, sent_and_summed(): parts = lax.all_to_all(cut_along(value, dim, size), axis, 0, 0, tiled=True)  11.5 us
  transfers between devices with their start and end apart: 2, of which 2 were waited for; matrix products, arithmetic and copies ran while one was open for 6% of the time, Pallas kernels for 0%

commit v1 on v0

--- a/solution.py
+++ b/solution.py
@@ -51,7 +51,9 @@
         back_list.append(out_back)
         gain_total = gain_total + by_axis(out_gain, DP_TENSOR)
     stacked = jnp.stack(back_list)
-    section = lax.all_gather(stacked, TENSOR, axis=1, tiled=True)
+    section = jnp.concatenate(
+        lax.all_to_all(jnp.stack([stacked] * lax.axis_size(TENSOR)), TENSOR, 0, 0), axis=1
+    )
     weight_sum = lax.dot_general(
         attention, section, (((0, 1), (0, 1)), ((), ())), preferred_element_type=jnp.float32
     )

time: 290 us -> 757 us (2.61)
  blocking collectives: 61.2 us -> 643 us
  waiting for transfers between devices: 161 us -> 11.8 us
  local copies, waits for them, and re-layouts: 0.2 us -> 38.7 us
  between operations: 14.1 us -> 0.73 us
  starting transfers between devices: 4.6 us -> 13.7 us
    psum x5, blocking collectives: 61.2 us -> 643 us  [by_axis(): return functools.reduce(lax.psum, axes, value)]
    all_gather x1 -> x0, waiting for transfers between devices: 149 us -> none  [per_device(): section = lax.all_gather(stacked, TENSOR, axis=1, tiled=True)]
    reshape x0 -> x1, local copies, waits for them, and re-layouts: none -> 25.8 us  [per_device(): jnp.concatenate(lax.all_to_all(jnp.stack([stacked] * lax.axis_size(TENSOR...]
    another operation x0 -> x1, local copies, waits for them, and re-layouts: none -> 12.7 us  [per_device(): jnp.stack([stacked] * lax.axis_size(TENSOR))]
    all_to_all x0 -> x1, starting transfers between devices: none -> 8.57 us  [per_device(): lax.all_to_all(jnp.stack([stacked] * lax.axis_size(TENSOR)), TENSOR, 0, 0)]
  transfers between devices with their start and end apart: 2 -> 2, of which waited for: 2 -> 1; matrix products, arithmetic and copies ran while one was open for 6% -> 2% of each run, Pallas kernels for 0% -> 0%
where the time goes in v1:
time: 757 us; the launch traced here: 756 us
  blocking collectives  643 us (85%)
  local copies, waits for them, and re-layouts  38.7 us (5%)
  matrix products  36.4 us (5%)
  starting transfers between devices  13.7 us (2%)
  waiting for transfers between devices  11.8 us (2%)
  other arithmetic  11.1 us (1%)
    psum x5, blocking collectives, by_axis(): return functools.reduce(lax.psum, axes, value)  643 us
    reshape x1, local copies, waits for them, and re-layouts, per_device(): jnp.concatenate(lax.all_to_all(jnp.stack([stacked] * lax.axis_size(TENSOR...  25.8 us
    dot_general x1, matrix products, per_device(): lax.dot_general(attention, section, (((0, 1), (0, 1)), ((), ())), preferr...  18.6 us
    dot_general x1, matrix products, per_device(): lax.dot_general(section, w_out, (((2,), (1,)), ((), ())), preferred_eleme...  17.7 us
  transfers between devices with their start and end apart: 2, of which 1 were waited for; matrix products, arithmetic and copies ran while one was open for 2% of the time, Pallas kernels for 0%

profile of v1, /device:TPU:1, one launch (start us, length us, event | category | flops | bytes accessed | tf_op | source)
XLA Modules:
  0.0 755.6 jit_solution(18152165219863923719)
XLA Ops:
  0.6 0.0 copy-start
  0.6 0.0 copy-start.1
  0.7 2.3 fusion.21
  3.0 0.2 copy-done.1
  3.2 0.0 copy-start.2
  3.2 0.0 copy-start.4
  3.2 3.5 fusion.12
  6.7 0.0 copy-done.2
  6.7 0.0 copy-done.4
  6.7 1.4 fusion.16
  8.1 0.2 pad_maximum_fusion
  8.3 12.7 %stack.5 = bf16[16,2,128,4608]{3,2,1,0:T(8,128)(2,1)} broadcast(bf16[2,128,4608]{2,1,0:T(8,128)(2,1)S(1)} %pad_maximum_fusion), dimensions={1,2,3} | broadcast | bytes 40108032 | tf_op jit(solution)/shard_map/stack | solution.py:55
  21.0 0.0 copy-start.5
  21.0 8.6 %all-to-all-start = ((bf16[16,2,128,4608]{3,2,1,0:T(8,128)(2,1)}), bf16[16,2,128,4608]{3,2,1,0:T(8,128)(2,1)}, u32[]{:S(2)}, u32[]{:S(2)}) async-start(bf16[16,2,128,4608]{3,2,1,0:T(8,128)(2,1)} %stack.5), calls=%async_computation | async-start | bytes 75497472 | tf_op jit(solution)/shard_map/all_to_all | solution.py:55
  29.6 16.1 %psum.84 = f32[4608]{0:T(1024)S(1)} all-reduce(f32[4608]{0:T(1024)S(1)} %add.48), channel_id=1, replica_groups=mesh['dp_0'=4,'dp_1'=2,'tensor_0'=4,'tensor_1'=2,'tensor_2'=2] {'dp_0'}, use_global_device_ids=true, to_apply=%region_6.0 | all-reduce | flops 4608 | bytes 36864 | tf_op jit(solution)/shard_map/psum | solution.py:15
  45.7 140.1 %psum.83 = f32[4608]{0:T(1024)S(1)} all-reduce(f32[4608]{0:T(1024)S(1)} %psum.84), channel_id=1, replica_groups=mesh['dp_0'=4,'dp_1'=2,'tensor_0'=4,'tensor_1'=2,'tensor_2'=2] {'dp_1'}, use_global_device_ids=true, to_apply=%region_7.0 | all-reduce | flops 4608 | bytes 36864 | tf_op jit(solution)/shard_map/psum | solution.py:15
  185.8 471.2 %psum.82 = f32[4608]{0:T(1024)S(1)} all-reduce(f32[4608]{0:T(1024)S(1)} %psum.83), channel_id=1, replica_groups=mesh['dp_0'=4,'dp_1'=2,'tensor_0'=4,'tensor_1'=2,'tensor_2'=2] {'tensor_0'}, use_global_device_ids=true, to_apply=%region_8.0 | all-reduce | flops 4608 | bytes 36864 | tf_op jit(solution)/shard_map/psum | solution.py:15
  657.1 6.6 psum.81
  663.7 9.2 %psum.80 = f32[4608]{0:T(1024)S(1)} all-reduce(f32[4608]{0:T(1024)S(1)} %psum.81), channel_id=1, replica_groups=mesh['dp_0'=4,'dp_1'=2,'tensor_0'=4,'tensor_1'=2,'tensor_2'=2] {'tensor_2'}, use_global_device_ids=true, to_apply=%region_10.0 | all-reduce | flops 4608 | bytes 36864 | tf_op jit(solution)/shard_map/psum | solution.py:15
  672.8 0.0 copy-done.5
  672.8 0.6 multiply_add_fusion.1
  673.4 0.0 all-to-all-done
  673.4 25.8 %copy.11 = bf16[2,16,128,4608]{3,2,1,0:T(8,128)(2,1)} copy(bf16[2,16,128,4608]{3,2,0,1:T(8,128)(2,1)} %bitcast.4) | data formatting | bytes 75497472 | tf_op jit(solution)/shard_map/reshape | solution.py:54
  699.3 18.6 %fusion = bf16[4608,256]{1,0:T(8,128)(2,1)} fusion(bf16[2,2048,4608]{2,1,0:T(8,128)(2,1)} %bitcast.69, bf16[2,2048,256]{2,1,0:T(8,128)(2,1)} %param.9), kind=kOutput, calls=%fused_computation.1 | convolution fusion | flops 9664856064 | bytes 42205184 | tf_op jit(solution)/shard_map/dot_general | solution.py:57
  717.9 5.1 all-to-all-start.1
  723.0 0.0 copy-done
  723.0 17.7 %convolution_convert_fusion = bf16[2,2048,256]{2,1,0:T(8,128)(2,1)} fusion(bf16[2,2048,4608]{2,1,0:T(8,128)(2,1)} %bitcast.70, bf16[256,4608]{1,0:T(8,128)(2,1)S(1)} %copy-done), kind=kOutput, calls=%fused_computation.3 | convolution fusion | flops 9664724992 | bytes 42205184 | tf_op jit(solution)/shard_map/dot_general | solution.py:60
  740.8 0.0 copy-start.3
  740.8 11.8 %all-to-all-done.1 = bf16[8,256,576]{1,2,0:T(8,128)(2,1)} async-done(((bf16[8,256,576]{1,2,0:T(8,128)(2,1)}), bf16[8,256,576]{1,2,0:T(8,128)(2,1)}, u32[]{:S(2)}, u32[]{:S(2)}) %all-to-all-start.1) | async-done | bytes 2359328 | tf_op jit(solution)/shard_map/all_to_all | solution.py:25
  752.6 2.0 convert_reduce_fusion
  754.6 0.0 copy-done.3
  754.6 0.9 multiply_add_fusion
  (4 shorter events, 0.0 us)
Async XLA Ops:
  0.6 722.4 %copy-start = (bf16[256,4608]{1,0:T(8,128)(2,1)S(1)}, bf16[256,4608]{1,0:T(8,128)(2,1)}, u32[]{:S(2)}) copy-start(bf16[256,4608]{1,0:T(8,128)(2,1)} %param.10) | copy-start | bytes 7077892
  0.6 2.5 copy-start.1
  3.2 3.5 copy-start.2
  3.2 3.5 copy-start.4
  21.0 651.8 %copy-start.5 = (f32[4608]{0:T(1024)S(1)}, f32[4608]{0:T(1024)}, u32[]{:S(2)}) copy-start(f32[4608]{0:T(1024)} %param.13) | copy-start | bytes 55300
  21.0 652.4 %all-to-all-start = ((bf16[16,2,128,4608]{3,2,1,0:T(8,128)(2,1)}), bf16[16,2,128,4608]{3,2,1,0:T(8,128)(2,1)}, u32[]{:S(2)}, u32[]{:S(2)}) async-start(bf16[16,2,128,4608]{3,2,1,0:T(8,128)(2,1)} %stack.5), calls=%async_computation | async-start | bytes 75497472 | tf_op jit(solution)/shard_map/all_to_all | solution.py:55
  717.9 34.7 %all-to-all-start.1 = ((bf16[8,256,576]{1,2,0:T(8,128)(2,1)}), bf16[8,256,576]{1,2,0:T(8,128)(2,1)}, u32[]{:S(2)}, u32[]{:S(2)}) async-start(bf16[8,256,576]{1,2,0:T(8,128)(2,1)} %bitcast.71), calls=%async_computation.1 | async-start | bytes 4718592 | tf_op jit(solution)/shard_map/all_to_all | solution.py:25
  740.8 13.8 %copy-start.3 = (f32[256,576]{0,1:T(8,128)S(1)}, f32[256,576]{0,1:T(8,128)}, u32[]{:S(2)}) copy-start(f32[256,576]{0,1:T(8,128)} %param.12) | copy-start | bytes 1769476
